TPU v7x, 32 devices: a whole 2x2x4 slice. The times are simulated.
32 devices in a mesh: slab: 4 (over x, core), patch: 8 (over z, y).
Axes of the slice: x: 2, y: 2, z: 4, core: 2. Of those that a mesh axis runs over, the one named last changes fastest.
Arguments:
- right_side: float32 [4, 8, 256, 768], P('slab', 'patch'), may hold values from -6 to 6
- inverse_factor: bfloat16 [4, 8, 768, 768], P('slab', 'patch'), may hold values from -0.12990381 to 1.5, as said below
- forward_trace: bfloat16 [4, 8, 128, 768], P('slab', 'patch'), may hold values from -0.375 to 0.375
- backward_trace: bfloat16 [4, 8, 128, 768], P('slab', 'patch'), may hold values from -0.375 to 0.375
- margin: int32 [4, 8], P('slab', 'patch'), may hold values from 1 to 256, as said below
Outputs:
- correction: float32 [4, 8, 256, 768], P('slab', 'patch')
Inputs may be any that keep to these rules, and one draw needn't show every extreme that they name: `inverse_factor`: lower triangular: zero above the diagonal, positive on it. margin[s, q] counts the last unknowns of patch q that are the first unknowns of patch q + 1 (of patch 0 for q = 7). In every slab some pair shares exactly 256.
All inputs are finite; a program needn't handle non-finite values.
Results may differ from a plain program's by a relative error of at most 0.035.
Values may be sent and summed in bfloat16 or wider, within the bound.
A program may use at most 64 MiB of HBM per device.

v0:
```python
import jax
import jax.numpy as jnp
from jax import lax
from jax.sharding import PartitionSpec as P

M = 768
KMAX = 256
FACE = 128


def from_behind(value, axis, steps):
    count = lax.axis_size(axis)
    pairs = [(source, (source + steps) % count) for source in range(count)]
    return lax.ppermute(value, axis, pairs)


def from_behind_2(array, axis, by):
    count = lax.axis_size(axis)
    pairs = [(i, i + by) for i in range(count) if 0 <= i + by < count]
    return lax.ppermute(array, axis, pairs)


def placement(counts):
    source_index = jnp.arange(KMAX, dtype=jnp.int32)[None, :, None]
    target_index = jnp.arange(KMAX, dtype=jnp.int32)[None, None, :]
    limit = counts[:, None, None]
    hit = (source_index == KMAX - limit + target_index) & (target_index < limit)
    return jnp.where(hit, 1.0, 0.0).astype(jnp.bfloat16)


def solve(values, factor):
    halfway = jnp.einsum(
        "pck,pik->pci", values.astype(jnp.bfloat16), factor, preferred_element_type=jnp.float32
    )
    return jnp.einsum(
        "pci,pik->pck", halfway.astype(jnp.bfloat16), factor, preferred_element_type=jnp.float32
    )


def slab_step(residual, factor, placing):
    initial = solve(residual, factor).astype(jnp.bfloat16)
    tail_rows = initial[:, :, M - KMAX :]
    head_rows = initial[:, :, :KMAX]
    placed = jnp.einsum(
        "pcs,psd->pcd", tail_rows, placing, preferred_element_type=jnp.float32
    ).astype(jnp.bfloat16)
    incoming = from_behind(placed, "patch", 1)
    from_left = jnp.concatenate([incoming, placed[:-1]], axis=0)
    beyond = from_behind(head_rows, "patch", -1)
    neighbours = jnp.concatenate([head_rows[1:], beyond], axis=0)
    from_right = jnp.einsum("pci,pti->pct", neighbours, placing, preferred_element_type=jnp.float32)
    middle = jnp.zeros((residual.shape[0], residual.shape[1], M - 2 * KMAX), jnp.float32)
    shared = jnp.concatenate([from_left.astype(jnp.float32), middle, from_right], axis=2)
    return solve(residual - 0.5 * shared, factor)


def face_map(matrix, corrected):
    return jnp.einsum(
        "pck,ptk->pct", corrected.astype(jnp.bfloat16), matrix, preferred_element_type=jnp.float32
    ).astype(jnp.bfloat16)


def face_terms(down_face, up_face):
    middle = jnp.zeros((down_face.shape[0], down_face.shape[1], M - 2 * FACE), jnp.float32)
    return jnp.concatenate(
        [down_face.astype(jnp.float32), middle, up_face.astype(jnp.float32)], axis=2
    )


def keep(store, fresh, active):
    return jnp.where(active, fresh, store)


def on_device(right_side, inverse_factor, forward_trace, backward_trace, margin):
    slab_index = lax.axis_index("slab")
    slab_count = lax.axis_size("slab")
    source = right_side[0]
    factor = inverse_factor[0]
    down_matrix = forward_trace[0]
    up_matrix = backward_trace[0]
    placing = placement(margin[0])
    patches = source.shape[0]
    columns = source.shape[1]
    blocks = columns // columns
    zero_face = jnp.zeros((patches, columns, FACE), jnp.bfloat16)

    def forward_section(section_index, carry):
        arriving, down_store, last_store, up_store = carry
        batch_index = section_index - slab_index
        active = (batch_index >= 0) & (batch_index < blocks)
        corrected = slab_step(source - face_terms(arriving, zero_face), factor, placing)
        down_store = keep(down_store, arriving, active)
        sending = face_map(down_matrix, corrected)
        arriving = from_behind_2(sending, "slab", 1)
        return (arriving, down_store, last_store, up_store)

    last_init = jnp.zeros((1,), jnp.float32)
    up_init = jnp.zeros((1,), jnp.bfloat16)
    down_init = jnp.zeros((patches, columns, FACE), jnp.bfloat16)
    carry = lax.fori_loop(
        0, slab_count + blocks - 1, forward_section, (zero_face, down_init, last_init, up_init)
    )
    down_store, last_store, up_store = (carry[1], carry[2], carry[3])
    lead = slab_count - 1
    sections = slab_count + blocks - 1

    def reverse_section(section_index, carry):
        pending, out_store = carry
        arriving = from_behind_2(pending, "slab", -1)
        batch_index = section_index - (lead - slab_index)
        active = (batch_index >= 0) & (batch_index < blocks)
        corrected = slab_step(source - face_terms(down_store, arriving), factor, placing)
        out_store = keep(out_store, corrected, active)
        pending = face_map(up_matrix, corrected)
        return (pending, out_store)

    out_init = jnp.zeros((patches, columns, M), jnp.float32)
    out_store = lax.fori_loop(0, sections, reverse_section, (zero_face, out_init))[1]
    return out_store[None]


def solution(mesh):
    placed = (
        P("slab", "patch", None, None),
        P("slab", "patch", None, None),
        P("slab", "patch", None, None),
        P("slab", "patch", None, None),
        P("slab", "patch"),
    )
    return jax.shard_map(
        on_device,
        mesh=mesh,
        in_specs=placed,
        out_specs=P("slab", "patch", None, None),
        check_vma=False,
    )
```

profile of v0, /device:TPU:0, one launch (start us, length us, event | category | flops | bytes accessed | tf_op | source)
XLA Modules:
  0.0 160.6 jit_solution(2775115109756332187)
XLA Ops:
  0.7 78.9 %while.34 = (s32[]{:T(128)}, bf16[1,256,128]{2,1,0:T(8,128)(2,1)S(1)}, bf16[1,256,128]{2,1,0:T(8,128)(2,1)S(1)}, f32[1,256,768]{2,1,0:T(8,128)}, bf16[1,768,768]...) while((s32[]{:T(128)}, ...), condition=%wide.region_1.2_spmd.clone, body=%wide.region_0.1_spmd.clone.sunk | while | flops 1329332224 | bytes 18311304 | solution.py:100
  3.7 6.1 %collective-permute-start = (bf16[1,256,256]{2,1,0:T(8,128)(2,1)S(1)}, bf16[1,256,256]{2,1,0:T(8,128)(2,1)S(1)}, u32[]{:S(2)}, u32[]{:S(2)}) collective-permute-start(bf16[1,256,256]{2,1,0:T(8,128)(2,1)S(1)} %slice.49), channel_id=1, source_target_pairs={{0,7},{1,0},{2,1},{3,2},{4,3},{5,4},{6,5},{7,6},{8,15},{9,8},{10,9... | collective-permute-start | bytes 393224 | tf_op jit(solution)/shard_map/while/body/eval_jaxpr/ppermute | solution.py:14
  13.5 4.2 %collective-permute-done.1 = bf16[1,256,256]{2,1,0:T(8,128)(2,1)S(1)} collective-permute-done((bf16[1,256,256]{2,1,0:T(8,128)(2,1)S(1)}, bf16[1,256,256]{2,1,0:T(8,128)(2,1)S(1)}, u32[]{:S(2)}, u32[]{:S(2)}) %collective-permute-start.1) | collective-permute-done | bytes 131104 | tf_op jit(solution)/shard_map/while/body/eval_jaxpr/ppermute | solution.py:14
  31.2 3.1 %collective-permute-done.1 = bf16[1,256,256]{2,1,0:T(8,128)(2,1)S(1)} collective-permute-done((bf16[1,256,256]{2,1,0:T(8,128)(2,1)S(1)}, bf16[1,256,256]{2,1,0:T(8,128)(2,1)S(1)}, u32[]{:S(2)}, u32[]{:S(2)}) %collective-permute-start.1) | collective-permute-done | bytes 131104 | tf_op jit(solution)/shard_map/while/body/eval_jaxpr/ppermute | solution.py:14
  36.6 3.1 %collective-permute-start.2 = (bf16[1,256,128]{2,1,0:T(8,128)(2,1)S(1)}, bf16[1,256,128]{2,1,0:T(8,128)(2,1)S(1)}, u32[]{:S(2)}, u32[]{:S(2)}) collective-permute-start(bf16[1,256,128]{2,1,0:T(8,128)(2,1)S(1)} %fusion.140), channel_id=1, source_target_pairs={{0,8},{8,16},{16,24},{1,9},{9,17},{17,25},{2,10},{10,18},{18,26},{... | collective-permute-start | bytes 196616 | tf_op jit(solution)/shard_map/while/body/eval_jaxpr/ppermute | solution.py:20
  40.7 2.9 %fusion.138 = bf16[1,256,768]{2,1,0:T(8,128)(2,1)S(1)} fusion(bf16[1,768,768]{2,1,0:T(8,128)(2,1)} %get-tuple-element.627, f32[1,256,768]{2,1,0:T(8,128)} %get-tuple-element.626, f32[1,256,128]{2,1,0:T(8,128)S(1)} %get-tuple-element.583, f32[768]{0:T(1024)S(1)} %pad.5.clone.2, f32[768]{0:T(1024)S(1)} %pad.4.clone.2), kind=kOutput, calls=%fused_computation.6.clone.1 | convolution fusion | flops 605159424 | bytes 2496512 | tf_op jit(solution)/shard_map/while/body/eval_jaxpr/pci,pik->pck/dot_general | solution.py:35
  49.5 3.1 %collective-permute-done.1 = bf16[1,256,256]{2,1,0:T(8,128)(2,1)S(1)} collective-permute-done((bf16[1,256,256]{2,1,0:T(8,128)(2,1)S(1)}, bf16[1,256,256]{2,1,0:T(8,128)(2,1)S(1)}, u32[]{:S(2)}, u32[]{:S(2)}) %collective-permute-start.1) | collective-permute-done | bytes 131104 | tf_op jit(solution)/shard_map/while/body/eval_jaxpr/ppermute | solution.py:14
  54.9 4.3 %collective-permute-start.2 = (bf16[1,256,128]{2,1,0:T(8,128)(2,1)S(1)}, bf16[1,256,128]{2,1,0:T(8,128)(2,1)S(1)}, u32[]{:S(2)}, u32[]{:S(2)}) collective-permute-start(bf16[1,256,128]{2,1,0:T(8,128)(2,1)S(1)} %fusion.140), channel_id=1, source_target_pairs={{0,8},{8,16},{16,24},{1,9},{9,17},{17,25},{2,10},{10,18},{18,26},{... | collective-permute-start | bytes 196616 | tf_op jit(solution)/shard_map/while/body/eval_jaxpr/ppermute | solution.py:20
  60.2 2.9 %fusion.138 = bf16[1,256,768]{2,1,0:T(8,128)(2,1)S(1)} fusion(bf16[1,768,768]{2,1,0:T(8,128)(2,1)} %get-tuple-element.627, f32[1,256,768]{2,1,0:T(8,128)} %get-tuple-element.626, f32[1,256,128]{2,1,0:T(8,128)S(1)} %get-tuple-element.583, f32[768]{0:T(1024)S(1)} %pad.5.clone.2, f32[768]{0:T(1024)S(1)} %pad.4.clone.2), kind=kOutput, calls=%fused_computation.6.clone.1 | convolution fusion | flops 605159424 | bytes 2496512 | tf_op jit(solution)/shard_map/while/body/eval_jaxpr/pci,pik->pck/dot_general | solution.py:35
  69.1 3.1 %collective-permute-done.1 = bf16[1,256,256]{2,1,0:T(8,128)(2,1)S(1)} collective-permute-done((bf16[1,256,256]{2,1,0:T(8,128)(2,1)S(1)}, bf16[1,256,256]{2,1,0:T(8,128)(2,1)S(1)}, u32[]{:S(2)}, u32[]{:S(2)}) %collective-permute-start.1) | collective-permute-done | bytes 131104 | tf_op jit(solution)/shard_map/while/body/eval_jaxpr/ppermute | solution.py:14
  74.5 4.3 %collective-permute-start.2 = (bf16[1,256,128]{2,1,0:T(8,128)(2,1)S(1)}, bf16[1,256,128]{2,1,0:T(8,128)(2,1)S(1)}, u32[]{:S(2)}, u32[]{:S(2)}) collective-permute-start(bf16[1,256,128]{2,1,0:T(8,128)(2,1)S(1)} %fusion.140), channel_id=1, source_target_pairs={{0,8},{8,16},{16,24},{1,9},{9,17},{17,25},{2,10},{10,18},{18,26},{... | collective-permute-start | bytes 196616 | tf_op jit(solution)/shard_map/while/body/eval_jaxpr/ppermute | solution.py:20
  79.7 80.9 %while.35 = (s32[]{:T(128)}, bf16[1,256,128]{2,1,0:T(8,128)(2,1)S(1)}, f32[1,256,768]{2,1,0:T(8,128)}, bf16[1,256,128]{2,1,0:T(8,128)(2,1)S(1)}, f32[1,256,768]{...) while((s32[]{:T(128)}, ...), condition=%wide.region_3.4_spmd.clone, body=%wide.region_2.3_spmd.clone.sunk | while | flops 1329692672 | bytes 19415156 | solution.py:118
  81.0 5.5 %collective-permute-done.3 = bf16[1,256,128]{2,1,0:T(8,128)(2,1)S(1)} collective-permute-done((bf16[1,256,128]{2,1,0:T(8,128)(2,1)S(1)}, bf16[1,256,128]{2,1,0:T(8,128)(2,1)S(1)}, u32[]{:S(2)}, u32[]{:S(2)}) %collective-permute-start.3) | collective-permute-done | bytes 65568 | tf_op jit(solution)/shard_map/while/body/eval_jaxpr/ppermute | solution.py:20
  86.6 2.9 %fusion.151 = bf16[1,256,768]{2,1,0:T(8,128)(2,1)S(1)} fusion(bf16[1,768,768]{2,1,0:T(8,128)(2,1)} %get-tuple-element.669, f32[1,256,768]{2,1,0:T(8,128)} %get-tuple-element.668, f32[1,256,128]{2,1,0:T(8,128)S(1)} %convert_element_type.443, f32[1,256,128]{2,1,0:T(8,128)S(1)} %convert_element_type.444, f32[768]{0:T(1024)S(1)} %pad.10.clone.2), kind=kOutput, calls=%fused_computation.49.clone.1 | convolution fusion | flops 605159424 | bytes 2624512 | tf_op jit(solution)/shard_map/while/body/eval_jaxpr/pci,pik->pck/dot_general | solution.py:35
  102.8 3.3 %collective-permute-done.3 = bf16[1,256,128]{2,1,0:T(8,128)(2,1)S(1)} collective-permute-done((bf16[1,256,128]{2,1,0:T(8,128)(2,1)S(1)}, bf16[1,256,128]{2,1,0:T(8,128)(2,1)S(1)}, u32[]{:S(2)}, u32[]{:S(2)}) %collective-permute-start.3) | collective-permute-done | bytes 65568 | tf_op jit(solution)/shard_map/while/body/eval_jaxpr/ppermute | solution.py:20
  106.1 2.9 %fusion.151 = bf16[1,256,768]{2,1,0:T(8,128)(2,1)S(1)} fusion(bf16[1,768,768]{2,1,0:T(8,128)(2,1)} %get-tuple-element.669, f32[1,256,768]{2,1,0:T(8,128)} %get-tuple-element.668, f32[1,256,128]{2,1,0:T(8,128)S(1)} %convert_element_type.443, f32[1,256,128]{2,1,0:T(8,128)S(1)} %convert_element_type.444, f32[768]{0:T(1024)S(1)} %pad.10.clone.2), kind=kOutput, calls=%fused_computation.49.clone.1 | convolution fusion | flops 605159424 | bytes 2624512 | tf_op jit(solution)/shard_map/while/body/eval_jaxpr/pci,pik->pck/dot_general | solution.py:35
  115.0 3.1 %collective-permute-done.5 = bf16[1,256,256]{2,1,0:T(8,128)(2,1)S(1)} collective-permute-done((bf16[1,256,256]{2,1,0:T(8,128)(2,1)S(1)}, bf16[1,256,256]{2,1,0:T(8,128)(2,1)S(1)}, u32[]{:S(2)}, u32[]{:S(2)}) %collective-permute-start.5) | collective-permute-done | bytes 131104 | tf_op jit(solution)/shard_map/while/body/eval_jaxpr/ppermute | solution.py:14
  118.2 3.1 %bitcast_select_fusion.2 = (f32[1,256,768]{2,1,0:T(8,128)}, bf16[256,768]{1,0:T(8,128)(2,1)S(1)}) fusion(f32[1,256,768]{2,1,0:T(8,128)} %get-tuple-element.652, pred[]{:T(512)S(6)} %compare.7, pred[]{:T(512)S(6)} %and.102, bf16[1,768,768]{2,1,0:T(8,128)(2,1)S(1)} %copy-done.3, f32[1,256,256]{2,1,0:T(8,128)} %convolution_bitcast_fusion.5, ...), kind=kOutput, calls=%fused_computation.62.clone.1 | convolution fusion | flops 606339072 | bytes 4983810 | tf_op jit(solution)/shard_map/while/body/eval_jaxpr/pci,pik->pck/dot_general | solution.py:35
  125.7 2.9 %fusion.151 = bf16[1,256,768]{2,1,0:T(8,128)(2,1)S(1)} fusion(bf16[1,768,768]{2,1,0:T(8,128)(2,1)} %get-tuple-element.669, f32[1,256,768]{2,1,0:T(8,128)} %get-tuple-element.668, f32[1,256,128]{2,1,0:T(8,128)S(1)} %convert_element_type.443, f32[1,256,128]{2,1,0:T(8,128)S(1)} %convert_element_type.444, f32[768]{0:T(1024)S(1)} %pad.10.clone.2), kind=kOutput, calls=%fused_computation.49.clone.1 | convolution fusion | flops 605159424 | bytes 2624512 | tf_op jit(solution)/shard_map/while/body/eval_jaxpr/pci,pik->pck/dot_general | solution.py:35
  134.6 3.1 %collective-permute-done.5 = bf16[1,256,256]{2,1,0:T(8,128)(2,1)S(1)} collective-permute-done((bf16[1,256,256]{2,1,0:T(8,128)(2,1)S(1)}, bf16[1,256,256]{2,1,0:T(8,128)(2,1)S(1)}, u32[]{:S(2)}, u32[]{:S(2)}) %collective-permute-start.5) | collective-permute-done | bytes 131104 | tf_op jit(solution)/shard_map/while/body/eval_jaxpr/ppermute | solution.py:14
  137.7 3.1 %bitcast_select_fusion.2 = (f32[1,256,768]{2,1,0:T(8,128)}, bf16[256,768]{1,0:T(8,128)(2,1)S(1)}) fusion(f32[1,256,768]{2,1,0:T(8,128)} %get-tuple-element.652, pred[]{:T(512)S(6)} %compare.7, pred[]{:T(512)S(6)} %and.102, bf16[1,768,768]{2,1,0:T(8,128)(2,1)S(1)} %copy-done.3, f32[1,256,256]{2,1,0:T(8,128)} %convolution_bitcast_fusion.5, ...), kind=kOutput, calls=%fused_computation.62.clone.1 | convolution fusion | flops 606339072 | bytes 4983810 | tf_op jit(solution)/shard_map/while/body/eval_jaxpr/pci,pik->pck/dot_general | solution.py:35
  145.3 2.9 %fusion.151 = bf16[1,256,768]{2,1,0:T(8,128)(2,1)S(1)} fusion(bf16[1,768,768]{2,1,0:T(8,128)(2,1)} %get-tuple-element.669, f32[1,256,768]{2,1,0:T(8,128)} %get-tuple-element.668, f32[1,256,128]{2,1,0:T(8,128)S(1)} %convert_element_type.443, f32[1,256,128]{2,1,0:T(8,128)S(1)} %convert_element_type.444, f32[768]{0:T(1024)S(1)} %pad.10.clone.2), kind=kOutput, calls=%fused_computation.49.clone.1 | convolution fusion | flops 605159424 | bytes 2624512 | tf_op jit(solution)/shard_map/while/body/eval_jaxpr/pci,pik->pck/dot_general | solution.py:35
  154.1 3.1 %collective-permute-done.5 = bf16[1,256,256]{2,1,0:T(8,128)(2,1)S(1)} collective-permute-done((bf16[1,256,256]{2,1,0:T(8,128)(2,1)S(1)}, bf16[1,256,256]{2,1,0:T(8,128)(2,1)S(1)}, u32[]{:S(2)}, u32[]{:S(2)}) %collective-permute-start.5) | collective-permute-done | bytes 131104 | tf_op jit(solution)/shard_map/while/body/eval_jaxpr/ppermute | solution.py:14
  157.3 3.1 %bitcast_select_fusion.2 = (f32[1,256,768]{2,1,0:T(8,128)}, bf16[256,768]{1,0:T(8,128)(2,1)S(1)}) fusion(f32[1,256,768]{2,1,0:T(8,128)} %get-tuple-element.652, pred[]{:T(512)S(6)} %compare.7, pred[]{:T(512)S(6)} %and.102, bf16[1,768,768]{2,1,0:T(8,128)(2,1)S(1)} %copy-done.3, f32[1,256,256]{2,1,0:T(8,128)} %convolution_bitcast_fusion.5, ...), kind=kOutput, calls=%fused_computation.62.clone.1 | convolution fusion | flops 606339072 | bytes 4983810 | tf_op jit(solution)/shard_map/while/body/eval_jaxpr/pci,pik->pck/dot_general | solution.py:35
  (174 shorter events, 82.9 us)
Async XLA Ops:
  3.7 8.8 %collective-permute-start = (bf16[1,256,256]{2,1,0:T(8,128)(2,1)S(1)}, bf16[1,256,256]{2,1,0:T(8,128)(2,1)S(1)}, u32[]{:S(2)}, u32[]{:S(2)}) collective-permute-start(bf16[1,256,256]{2,1,0:T(8,128)(2,1)S(1)} %slice.49), channel_id=1, source_target_pairs={{0,7},{1,0},{2,1},{3,2},{4,3},{5,4},{6,5},{7,6},{8,15},{9,8},{10,9... | collective-permute-start | bytes 393224 | tf_op jit(solution)/shard_map/while/body/eval_jaxpr/ppermute | solution.py:14
  10.0 7.7 %collective-permute-start.1 = (bf16[1,256,256]{2,1,0:T(8,128)(2,1)S(1)}, bf16[1,256,256]{2,1,0:T(8,128)(2,1)S(1)}, u32[]{:S(2)}, u32[]{:S(2)}) collective-permute-start(bf16[1,256,256]{2,1,0:T(8,128)(2,1)S(1)} %fusion.139), channel_id=1, source_target_pairs={{0,1},{1,2},{2,3},{3,4},{4,5},{5,6},{6,7},{7,0},{8,9},{9,10},{10,1... | collective-permute-start | bytes 393224 | tf_op jit(solution)/shard_map/while/body/eval_jaxpr/ppermute | solution.py:14
  20.1 2.2 %collective-permute-start.2 = (bf16[1,256,128]{2,1,0:T(8,128)(2,1)S(1)}, bf16[1,256,128]{2,1,0:T(8,128)(2,1)S(1)}, u32[]{:S(2)}, u32[]{:S(2)}) collective-permute-start(bf16[1,256,128]{2,1,0:T(8,128)(2,1)S(1)} %fusion.140), channel_id=1, source_target_pairs={{0,8},{8,16},{16,24},{1,9},{9,17},{17,25},{2,10},{10,18},{18,26},{... | collective-permute-start | bytes 196616 | tf_op jit(solution)/shard_map/while/body/eval_jaxpr/ppermute | solution.py:20
  25.2 5.0 %collective-permute-start = (bf16[1,256,256]{2,1,0:T(8,128)(2,1)S(1)}, bf16[1,256,256]{2,1,0:T(8,128)(2,1)S(1)}, u32[]{:S(2)}, u32[]{:S(2)}) collective-permute-start(bf16[1,256,256]{2,1,0:T(8,128)(2,1)S(1)} %slice.49), channel_id=1, source_target_pairs={{0,7},{1,0},{2,1},{3,2},{4,3},{5,4},{6,5},{7,6},{8,15},{9,8},{10,9... | collective-permute-start | bytes 393224 | tf_op jit(solution)/shard_map/while/body/eval_jaxpr/ppermute | solution.py:14
  26.5 7.7 %collective-permute-start.1 = (bf16[1,256,256]{2,1,0:T(8,128)(2,1)S(1)}, bf16[1,256,256]{2,1,0:T(8,128)(2,1)S(1)}, u32[]{:S(2)}, u32[]{:S(2)}) collective-permute-start(bf16[1,256,256]{2,1,0:T(8,128)(2,1)S(1)} %fusion.139), channel_id=1, source_target_pairs={{0,1},{1,2},{2,3},{3,4},{4,5},{5,6},{6,7},{7,0},{8,9},{9,10},{10,1... | collective-permute-start | bytes 393224 | tf_op jit(solution)/shard_map/while/body/eval_jaxpr/ppermute | solution.py:14
  36.6 4.0 %collective-permute-start.2 = (bf16[1,256,128]{2,1,0:T(8,128)(2,1)S(1)}, bf16[1,256,128]{2,1,0:T(8,128)(2,1)S(1)}, u32[]{:S(2)}, u32[]{:S(2)}) collective-permute-start(bf16[1,256,128]{2,1,0:T(8,128)(2,1)S(1)} %fusion.140), channel_id=1, source_target_pairs={{0,8},{8,16},{16,24},{1,9},{9,17},{17,25},{2,10},{10,18},{18,26},{... | collective-permute-start | bytes 196616 | tf_op jit(solution)/shard_map/while/body/eval_jaxpr/ppermute | solution.py:20
  43.6 5.0 %collective-permute-start = (bf16[1,256,256]{2,1,0:T(8,128)(2,1)S(1)}, bf16[1,256,256]{2,1,0:T(8,128)(2,1)S(1)}, u32[]{:S(2)}, u32[]{:S(2)}) collective-permute-start(bf16[1,256,256]{2,1,0:T(8,128)(2,1)S(1)} %slice.49), channel_id=1, source_target_pairs={{0,7},{1,0},{2,1},{3,2},{4,3},{5,4},{6,5},{7,6},{8,15},{9,8},{10,9... | collective-permute-start | bytes 393224 | tf_op jit(solution)/shard_map/while/body/eval_jaxpr/ppermute | solution.py:14
  44.8 7.8 %collective-permute-start.1 = (bf16[1,256,256]{2,1,0:T(8,128)(2,1)S(1)}, bf16[1,256,256]{2,1,0:T(8,128)(2,1)S(1)}, u32[]{:S(2)}, u32[]{:S(2)}) collective-permute-start(bf16[1,256,256]{2,1,0:T(8,128)(2,1)S(1)} %fusion.139), channel_id=1, source_target_pairs={{0,1},{1,2},{2,3},{3,4},{4,5},{5,6},{6,7},{7,0},{8,9},{9,10},{10,1... | collective-permute-start | bytes 393224 | tf_op jit(solution)/shard_map/while/body/eval_jaxpr/ppermute | solution.py:14
  54.9 5.2 %collective-permute-start.2 = (bf16[1,256,128]{2,1,0:T(8,128)(2,1)S(1)}, bf16[1,256,128]{2,1,0:T(8,128)(2,1)S(1)}, u32[]{:S(2)}, u32[]{:S(2)}) collective-permute-start(bf16[1,256,128]{2,1,0:T(8,128)(2,1)S(1)} %fusion.140), channel_id=1, source_target_pairs={{0,8},{8,16},{16,24},{1,9},{9,17},{17,25},{2,10},{10,18},{18,26},{... | collective-permute-start | bytes 196616 | tf_op jit(solution)/shard_map/while/body/eval_jaxpr/ppermute | solution.py:20
  63.1 5.0 %collective-permute-start = (bf16[1,256,256]{2,1,0:T(8,128)(2,1)S(1)}, bf16[1,256,256]{2,1,0:T(8,128)(2,1)S(1)}, u32[]{:S(2)}, u32[]{:S(2)}) collective-permute-start(bf16[1,256,256]{2,1,0:T(8,128)(2,1)S(1)} %slice.49), channel_id=1, source_target_pairs={{0,7},{1,0},{2,1},{3,2},{4,3},{5,4},{6,5},{7,6},{8,15},{9,8},{10,9... | collective-permute-start | bytes 393224 | tf_op jit(solution)/shard_map/while/body/eval_jaxpr/ppermute | solution.py:14
  64.3 7.8 %collective-permute-start.1 = (bf16[1,256,256]{2,1,0:T(8,128)(2,1)S(1)}, bf16[1,256,256]{2,1,0:T(8,128)(2,1)S(1)}, u32[]{:S(2)}, u32[]{:S(2)}) collective-permute-start(bf16[1,256,256]{2,1,0:T(8,128)(2,1)S(1)} %fusion.139), channel_id=1, source_target_pairs={{0,1},{1,2},{2,3},{3,4},{4,5},{5,6},{6,7},{7,0},{8,9},{9,10},{10,1... | collective-permute-start | bytes 393224 | tf_op jit(solution)/shard_map/while/body/eval_jaxpr/ppermute | solution.py:14
  74.5 5.2 %collective-permute-start.2 = (bf16[1,256,128]{2,1,0:T(8,128)(2,1)S(1)}, bf16[1,256,128]{2,1,0:T(8,128)(2,1)S(1)}, u32[]{:S(2)}, u32[]{:S(2)}) collective-permute-start(bf16[1,256,128]{2,1,0:T(8,128)(2,1)S(1)} %fusion.140), channel_id=1, source_target_pairs={{0,8},{8,16},{16,24},{1,9},{9,17},{17,25},{2,10},{10,18},{18,26},{... | collective-permute-start | bytes 196616 | tf_op jit(solution)/shard_map/while/body/eval_jaxpr/ppermute | solution.py:20
  79.7 6.9 %collective-permute-start.3 = (bf16[1,256,128]{2,1,0:T(8,128)(2,1)S(1)}, bf16[1,256,128]{2,1,0:T(8,128)(2,1)S(1)}, u32[]{:S(2)}, u32[]{:S(2)}) collective-permute-start(bf16[1,256,128]{2,1,0:T(8,128)(2,1)S(1)} %get-tuple-element.651), channel_id=1, source_target_pairs={{8,0},{16,8},{24,16},{9,1},{17,9},{25,17},{10,2},{18,10},{26,18},{... | collective-permute-start | bytes 196616 | tf_op jit(solution)/shard_map/while/body/eval_jaxpr/ppermute | solution.py:20
  89.5 5.0 %collective-permute-start.4 = (bf16[1,256,256]{2,1,0:T(8,128)(2,1)S(1)}, bf16[1,256,256]{2,1,0:T(8,128)(2,1)S(1)}, u32[]{:S(2)}, u32[]{:S(2)}) collective-permute-start(bf16[1,256,256]{2,1,0:T(8,128)(2,1)S(1)} %slice.51), channel_id=1, source_target_pairs={{0,7},{1,0},{2,1},{3,2},{4,3},{5,4},{6,5},{7,6},{8,15},{9,8},{10,9... | collective-permute-start | bytes 393224 | tf_op jit(solution)/shard_map/while/body/eval_jaxpr/ppermute | solution.py:14
  90.5 7.8 %collective-permute-start.5 = (bf16[1,256,256]{2,1,0:T(8,128)(2,1)S(1)}, bf16[1,256,256]{2,1,0:T(8,128)(2,1)S(1)}, u32[]{:S(2)}, u32[]{:S(2)}) collective-permute-start(bf16[1,256,256]{2,1,0:T(8,128)(2,1)S(1)} %fusion.152), channel_id=1, source_target_pairs={{0,1},{1,2},{2,3},{3,4},{4,5},{5,6},{6,7},{7,0},{8,9},{9,10},{10,1... | collective-permute-start | bytes 393224 | tf_op jit(solution)/shard_map/while/body/eval_jaxpr/ppermute | solution.py:14
  101.4 4.7 %collective-permute-start.3 = (bf16[1,256,128]{2,1,0:T(8,128)(2,1)S(1)}, bf16[1,256,128]{2,1,0:T(8,128)(2,1)S(1)}, u32[]{:S(2)}, u32[]{:S(2)}) collective-permute-start(bf16[1,256,128]{2,1,0:T(8,128)(2,1)S(1)} %get-tuple-element.651), channel_id=1, source_target_pairs={{8,0},{16,8},{24,16},{9,1},{17,9},{25,17},{10,2},{18,10},{26,18},{... | collective-permute-start | bytes 196616 | tf_op jit(solution)/shard_map/while/body/eval_jaxpr/ppermute | solution.py:20
  109.1 5.0 %collective-permute-start.4 = (bf16[1,256,256]{2,1,0:T(8,128)(2,1)S(1)}, bf16[1,256,256]{2,1,0:T(8,128)(2,1)S(1)}, u32[]{:S(2)}, u32[]{:S(2)}) collective-permute-start(bf16[1,256,256]{2,1,0:T(8,128)(2,1)S(1)} %slice.51), channel_id=1, source_target_pairs={{0,7},{1,0},{2,1},{3,2},{4,3},{5,4},{6,5},{7,6},{8,15},{9,8},{10,9... | collective-permute-start | bytes 393224 | tf_op jit(solution)/shard_map/while/body/eval_jaxpr/ppermute | solution.py:14
  110.4 7.7 %collective-permute-start.5 = (bf16[1,256,256]{2,1,0:T(8,128)(2,1)S(1)}, bf16[1,256,256]{2,1,0:T(8,128)(2,1)S(1)}, u32[]{:S(2)}, u32[]{:S(2)}) collective-permute-start(bf16[1,256,256]{2,1,0:T(8,128)(2,1)S(1)} %fusion.152), channel_id=1, source_target_pairs={{0,1},{1,2},{2,3},{3,4},{4,5},{5,6},{6,7},{7,0},{8,9},{9,10},{10,1... | collective-permute-start | bytes 393224 | tf_op jit(solution)/shard_map/while/body/eval_jaxpr/ppermute | solution.py:14
  121.5 4.2 %collective-permute-start.3 = (bf16[1,256,128]{2,1,0:T(8,128)(2,1)S(1)}, bf16[1,256,128]{2,1,0:T(8,128)(2,1)S(1)}, u32[]{:S(2)}, u32[]{:S(2)}) collective-permute-start(bf16[1,256,128]{2,1,0:T(8,128)(2,1)S(1)} %get-tuple-element.651), channel_id=1, source_target_pairs={{8,0},{16,8},{24,16},{9,1},{17,9},{25,17},{10,2},{18,10},{26,18},{... | collective-permute-start | bytes 196616 | tf_op jit(solution)/shard_map/while/body/eval_jaxpr/ppermute | solution.py:20
  128.6 5.0 %collective-permute-start.4 = (bf16[1,256,256]{2,1,0:T(8,128)(2,1)S(1)}, bf16[1,256,256]{2,1,0:T(8,128)(2,1)S(1)}, u32[]{:S(2)}, u32[]{:S(2)}) collective-permute-start(bf16[1,256,256]{2,1,0:T(8,128)(2,1)S(1)} %slice.51), channel_id=1, source_target_pairs={{0,7},{1,0},{2,1},{3,2},{4,3},{5,4},{6,5},{7,6},{8,15},{9,8},{10,9... | collective-permute-start | bytes 393224 | tf_op jit(solution)/shard_map/while/body/eval_jaxpr/ppermute | solution.py:14
  129.9 7.7 %collective-permute-start.5 = (bf16[1,256,256]{2,1,0:T(8,128)(2,1)S(1)}, bf16[1,256,256]{2,1,0:T(8,128)(2,1)S(1)}, u32[]{:S(2)}, u32[]{:S(2)}) collective-permute-start(bf16[1,256,256]{2,1,0:T(8,128)(2,1)S(1)} %fusion.152), channel_id=1, source_target_pairs={{0,1},{1,2},{2,3},{3,4},{4,5},{5,6},{6,7},{7,0},{8,9},{9,10},{10,1... | collective-permute-start | bytes 393224 | tf_op jit(solution)/shard_map/while/body/eval_jaxpr/ppermute | solution.py:14
  141.1 4.2 %collective-permute-start.3 = (bf16[1,256,128]{2,1,0:T(8,128)(2,1)S(1)}, bf16[1,256,128]{2,1,0:T(8,128)(2,1)S(1)}, u32[]{:S(2)}, u32[]{:S(2)}) collective-permute-start(bf16[1,256,128]{2,1,0:T(8,128)(2,1)S(1)} %get-tuple-element.651), channel_id=1, source_target_pairs={{8,0},{16,8},{24,16},{9,1},{17,9},{25,17},{10,2},{18,10},{26,18},{... | collective-permute-start | bytes 196616 | tf_op jit(solution)/shard_map/while/body/eval_jaxpr/ppermute | solution.py:20
  148.2 5.0 %collective-permute-start.4 = (bf16[1,256,256]{2,1,0:T(8,128)(2,1)S(1)}, bf16[1,256,256]{2,1,0:T(8,128)(2,1)S(1)}, u32[]{:S(2)}, u32[]{:S(2)}) collective-permute-start(bf16[1,256,256]{2,1,0:T(8,128)(2,1)S(1)} %slice.51), channel_id=1, source_target_pairs={{0,7},{1,0},{2,1},{3,2},{4,3},{5,4},{6,5},{7,6},{8,15},{9,8},{10,9... | collective-permute-start | bytes 393224 | tf_op jit(solution)/shard_map/while/body/eval_jaxpr/ppermute | solution.py:14
  149.5 7.7 %collective-permute-start.5 = (bf16[1,256,256]{2,1,0:T(8,128)(2,1)S(1)}, bf16[1,256,256]{2,1,0:T(8,128)(2,1)S(1)}, u32[]{:S(2)}, u32[]{:S(2)}) collective-permute-start(bf16[1,256,256]{2,1,0:T(8,128)(2,1)S(1)} %fusion.152), channel_id=1, source_target_pairs={{0,1},{1,2},{2,3},{3,4},{4,5},{5,6},{6,7},{7,0},{8,9},{9,10},{10,1... | collective-permute-start | bytes 393224 | tf_op jit(solution)/shard_map/while/body/eval_jaxpr/ppermute | solution.py:14
  (21 other events, 265.3 us)
where the time goes:
time: 162 us; the launch traced here: 161 us
  waiting for transfers between devices  64.9 us (40%)
  matrix products  53.9 us (33%)
  starting transfers between devices  39.3 us (24%)
    ppermute x16, waiting for transfers between devices, from_behind(): return lax.ppermute(value, axis, pairs)  46.8 us
    dot_general x16, matrix products, solve(): jnp.einsum('pci,pik->pck', halfway.astype(jnp.bfloat16), factor, preferre...  42.8 us
    ppermute x16, starting transfers between devices, from_behind(): return lax.ppermute(value, axis, pairs)  21.1 us
    ppermute x8, starting transfers between devices, from_behind_2(): return lax.ppermute(array, axis, pairs)  18.2 us
    ppermute x8, waiting for transfers between devices, from_behind_2(): return lax.ppermute(array, axis, pairs)  18 us
    dot_general x8, matrix products, slab_step(): jnp.einsum('pci,pti->pct', neighbours, placing, preferred_element_type=jn...  7.42 us
  transfers between devices with their start and end apart: 24, of which 24 were waited for; matrix products, arithmetic and copies ran while one was open for 6% of the time, Pallas kernels for 0%

commit v1 on v0

v1 whole, which is shorter than its diff:
```python
import functools

import jax
import jax.numpy as jnp
from jax import lax
from jax.experimental import pallas as pl
from jax.experimental.pallas import tpu as pltpu
from jax.sharding import PartitionSpec as P

KMAX = 256
BF = jnp.bfloat16
F32 = jnp.float32
MESH = pl.DeviceIdType.MESH


def nt(a, b):
    return lax.dot_general(a, b, (((1,), (1,)), ((), ())), preferred_element_type=F32)


def nn(a, b):
    return lax.dot_general(a, b, (((1,), (0,)), ((), ())), preferred_element_type=F32)


def tn(a, b):
    return lax.dot_general(a, b, (((0,), (0,)), ((), ())), preferred_element_type=F32)


def solve(x, fac, m):
    half = jnp.concatenate(
        [nt(x[:, : i + KMAX], fac[i : i + KMAX, : i + KMAX]).astype(BF) for i in range(0, m, KMAX)],
        axis=1,
    )
    return [nn(half[:, k:], fac[k:, k : k + KMAX]) for k in range(0, m, KMAX)]


def kernel(
    slabs, patches,
    r_ref, l_ref, f_ref, b_ref, margin_ref, out_ref,
    tail_s, head_s, zt_s, zh_s, d_s, u_s,
    tail_r, head_r, zt_r, zh_r, d_r, u_r,
    adj, acc, gt, opd, opu, place, zr,
    send_sem, recv_sem,
):
    s = lax.axis_index("slab")
    q = lax.axis_index("patch")
    left = lax.rem(q + patches - 1, patches)
    right = lax.rem(q + 1, patches)
    around = (q, left, right)
    m = l_ref.shape[-1]
    face = f_ref.shape[-2]
    fac = l_ref.at[0, 0]

    barrier = pltpu.get_barrier_semaphore()

    def greet(slab, patch):
        pl.semaphore_signal(barrier, inc=1, device_id=(slab, patch), device_id_type=MESH)

    greet(s, left)
    greet(s, right)

    @pl.when(s > 0)
    def _():
        for p in around:
            greet(s - 1, p)

    @pl.when(s < slabs - 1)
    def _():
        for p in around:
            greet(s + 1, p)

    def send(src, dst, slot_from, slot_to, slab, patch):
        return pltpu.make_async_remote_copy(
            src_ref=src, dst_ref=dst, send_sem=send_sem.at[slot_from], recv_sem=recv_sem.at[slot_to],
            device_id=(slab, patch), device_id_type=MESH,
        )

    tail_c = send(tail_s, tail_r, 0, 0, s, right)
    head_c = send(head_s, head_r, 1, 1, s, left)
    zt_c = send(zt_s, zt_r, 2, 2, s, right)
    zh_c = send(zh_s, zh_r, 3, 3, s, left)
    down_c = [send(d_s, d_r.at[j], 4 + j, 4 + j, s + 1, p) for j, p in ((0, q), (2, left), (1, right))]
    up_c = [send(u_s, u_r.at[j], 7 + j, 7 + j, s - 1, p) for j, p in ((0, q), (2, left), (1, right))]

    count = margin_ref[0, 0]
    row = lax.broadcasted_iota(jnp.int32, (KMAX, KMAX), 0)
    col = lax.broadcasted_iota(jnp.int32, (KMAX, KMAX), 1)
    hit = (row == KMAX - count + col) & (col < count)
    place[...] = jnp.where(hit, 1.0, 0.0).astype(BF)

    first = solve(r_ref[0, 0].astype(BF), fac, m)
    tail_s[...] = nn(first[-1].astype(BF), place[...]).astype(BF)
    head_s[...] = first[0].astype(BF)

    pl.semaphore_wait(barrier, 2 + 3 * (s > 0).astype(jnp.int32) + 3 * (s < slabs - 1).astype(jnp.int32))
    tail_c.start()
    head_c.start()

    low = fac[:, :face]
    high = fac[m - face :, m - face :]
    k_tail = jnp.concatenate(
        [tn(low[m - KMAX :], fac[m - KMAX :, m - KMAX :]), tn(high, fac[m - face :, m - KMAX :])], axis=0
    )
    k_head = jnp.concatenate([tn(low, fac[:, :KMAX]), tn(high, fac[m - face :, :KMAX])], axis=0)
    zt_s[...] = nn(k_tail.astype(BF), place[...]).astype(BF)
    zh_s[...] = k_head.astype(BF)
    zt_c.start()
    zh_c.start()

    maps = jnp.concatenate([f_ref[0, 0], b_ref[0, 0]], axis=0)
    for k, part in enumerate(solve(maps, fac, m)):
        gt[:, k * KMAX : (k + 1) * KMAX] = part.astype(BF)

    tail_c.wait_recv()
    head_c.wait_recv()
    adj[...] = r_ref[0, 0]
    adj[:, :KMAX] = adj[:, :KMAX] - 0.5 * tail_r[...].astype(F32)
    adj[:, m - KMAX :] = adj[:, m - KMAX :] - 0.5 * nt(head_r[...], place[...])
    acc[...] = nt(adj[...].astype(BF), gt[...])

    def send_down():
        d_s[...] = acc[:, :face].astype(BF)
        for c in down_c:
            c.start()

    def send_up():
        u_s[...] = acc[:, face:].astype(BF)
        for c in up_c:
            c.start()

    @pl.when(s == 0)
    def _():
        send_down()

    zt_c.wait_recv()
    zh_c.wait_recv()
    zr[...] = nt(zh_r[...], place[...]).astype(BF)
    op_l = (0.5 * nt(gt[:, :KMAX], zt_r[...])).astype(BF)
    op_r = (0.5 * nt(gt[:, m - KMAX :], zr[...])).astype(BF)
    opd[:, :face] = -gt[:, :face]
    opd[:, face : 2 * face] = op_l[:, :face]
    opd[:, 2 * face :] = op_r[:, :face]
    opu[:, :face] = -gt[face:, m - face :]
    opu[:, face : 2 * face] = op_l[face:, face:]
    opu[:, 2 * face :] = op_r[face:, face:]

    def beside(ref):
        return jnp.concatenate([ref[0], ref[1], ref[2]], axis=1)

    @pl.when(s > 0)
    def _():
        for c in down_c:
            c.wait_recv()
        acc[...] += nt(beside(d_r), opd[...])

        @pl.when(s < slabs - 1)
        def _():
            send_down()

        @pl.when(s == slabs - 1)
        def _():
            send_up()

        adj[:, :face] = adj[:, :face] - d_r[0].astype(F32)
        adj[:, :KMAX] = adj[:, :KMAX] + 0.5 * nn(d_r[1], zt_r[:face])
        adj[:, m - KMAX :] = adj[:, m - KMAX :] + 0.5 * nn(d_r[2], zr[:face])

    @pl.when(s < slabs - 1)
    def _():
        for c in up_c:
            c.wait_recv()

        @pl.when(s > 0)
        def _():
            acc[:, face:] = acc[:, face:] + nt(beside(u_r), opu[...])
            send_up()

        adj[:, m - face :] = adj[:, m - face :] - u_r[0].astype(F32)
        adj[:, :KMAX] = adj[:, :KMAX] + 0.5 * nn(u_r[1], zt_r[face:])
        adj[:, m - KMAX :] = adj[:, m - KMAX :] + 0.5 * nn(u_r[2], zr[face:])

    for k, part in enumerate(solve(adj[...].astype(BF), fac, m)):
        out_ref[0, 0, :, k * KMAX : (k + 1) * KMAX] = part

    for c in (tail_c, head_c, zt_c, zh_c):
        c.wait_send()

    @pl.when(s < slabs - 1)
    def _():
        for c in down_c:
            c.wait_send()

    @pl.when(s > 0)
    def _():
        for c in up_c:
            c.wait_send()


def on_device(slabs, patches, right_side, inverse_factor, forward_trace, backward_trace, margin):
    cols, m = right_side.shape[2:]
    face = forward_trace.shape[2]
    wide = pltpu.VMEM((cols, KMAX), BF)
    square = pltpu.VMEM((2 * face, KMAX), BF)
    thin = pltpu.VMEM((cols, face), BF)
    three = pltpu.VMEM((3, cols, face), BF)
    vm = pl.BlockSpec(memory_space=pltpu.VMEM)
    return pl.pallas_call(
        functools.partial(kernel, slabs, patches),
        out_shape=jax.ShapeDtypeStruct(right_side.shape, F32),
        in_specs=[vm, vm, vm, vm, pl.BlockSpec(memory_space=pltpu.SMEM)],
        out_specs=vm,
        scratch_shapes=[
            wide, wide, square, square, thin, thin,
            wide, wide, square, square, three, three,
            pltpu.VMEM((cols, m), F32),
            pltpu.VMEM((cols, 2 * face), F32),
            pltpu.VMEM((2 * face, m), BF),
            pltpu.VMEM((2 * face, 3 * face), BF),
            pltpu.VMEM((face, 3 * face), BF),
            pltpu.VMEM((KMAX, KMAX), BF),
            square,
            pltpu.SemaphoreType.DMA((10,)),
            pltpu.SemaphoreType.DMA((10,)),
        ],
        compiler_params=pltpu.CompilerParams(collective_id=0, has_side_effects=True),
        name="sweeps",
    )(right_side, inverse_factor, forward_trace, backward_trace, margin)


def solution(mesh):
    four = P("slab", "patch", None, None)
    return jax.shard_map(
        functools.partial(on_device, mesh.shape["slab"], mesh.shape["patch"]),
        mesh=mesh,
        in_specs=(four, four, four, four, P("slab", "patch")),
        out_specs=four,
        check_vma=False,
    )
```

time: 162 us -> 49.1 us (0.30)
  waiting for transfers between devices: 64.9 us -> 0 us
  matrix products: 53.9 us -> 0 us
  Pallas kernels: 0 us -> 46.1 us
  starting transfers between devices: 39.3 us -> 0 us
    ppermute x24 -> x0, waiting for transfers between devices: 64.9 us -> none  [the longest x16 46.8 us: from_behind(): return lax.ppermute(value, axis, pairs)]
    dot_general x40 -> x0, matrix products: 53.9 us -> none  [the longest x16 42.8 us: solve(): jnp.einsum('pci,pik->pck', halfway.astype(jnp.bfloat16), factor, preferre...]
    pallas_call x0 -> x1, Pallas kernels: none -> 46.1 us  [on_device(): pl.pallas_call(functools.partial(kernel, slabs, patches), out_shape=jax.S...]
    ppermute x24 -> x0, starting transfers between devices: 39.3 us -> none  [the longest x16 21.1 us: from_behind(): return lax.ppermute(value, axis, pairs)]
    unnamed x2 -> x1, local copies, waits for them, and re-layouts: 0.01 us -> 2.06 us
  transfers between devices with their start and end apart: 24 -> 0, of which waited for: 24 -> 0; matrix products, arithmetic and copies ran while one was open for 6% -> 0% of each run, Pallas kernels for 0% -> 0%
where the time goes in v1:
time: 49.1 us; the launch traced here: 48.9 us
  Pallas kernels  46.1 us (94%)
  local copies, waits for them, and re-layouts  2.06 us (4%)
  between operations  0.66 us (1%)
    pallas_call x1, Pallas kernels, on_device(): pl.pallas_call(functools.partial(kernel, slabs, patches), out_shape=jax.S...  46.1 us
    unnamed x1, local copies, waits for them, and re-layouts  2.06 us

profile of v1, /device:TPU:0, one launch (start us, length us, event | category | flops | bytes accessed | tf_op | source)
XLA Modules:
  0.0 48.9 jit_solution(2892325858306281099)
XLA Ops:
  0.7 46.1 %sweeps.1 = f32[1,1,256,768]{3,2,1,0:T(8,128)} custom-call(f32[1,1,256,768]{3,2,1,0:T(8,128)} %r_ref.1, bf16[1,1,768,768]{3,2,1,0:T(8,128)(2,1)} %l_ref.1, bf16[1,1,128,768]{3,2,1,0:T(8,128)(2,1)} %f_ref.1, bf16[1,1,128,768]{3,2,1,0:T(8,128)(2,1)} %b_ref.1, s32[1,1]{1,0:T(1,128)S(6)} %copy.7.margin_ref), custom_call_target="tpu_custom_call" | custom-call | tf_op jit(solution)/shard_map/sweeps/pallas_call | solution.py:206
  46.8 2.1 %copy.8 = f32[1,1,256,768]{3,2,1,0:T(8,128)} copy(f32[1,1,256,768]{3,2,1,0:T(8,128)} %sweeps.1) | data formatting | bytes 1572864

commit v2 on v1

v2 whole, which is shorter than its diff:
```python
import functools

import jax
import jax.numpy as jnp
from jax import lax
from jax.experimental import pallas as pl
from jax.experimental.pallas import tpu as pltpu
from jax.sharding import PartitionSpec as P

KMAX = 256
BF = jnp.bfloat16
F32 = jnp.float32
MESH = pl.DeviceIdType.MESH


def nt(a, b):
    return lax.dot_general(a, b, (((1,), (1,)), ((), ())), preferred_element_type=F32)


def nn(a, b):
    return lax.dot_general(a, b, (((1,), (0,)), ((), ())), preferred_element_type=F32)


def tn(a, b):
    return lax.dot_general(a, b, (((0,), (0,)), ((), ())), preferred_element_type=F32)


def solve(x, fac, m):
    half = jnp.concatenate(
        [nt(x[:, : i + KMAX], fac[i : i + KMAX, : i + KMAX]).astype(BF) for i in range(0, m, KMAX)],
        axis=1,
    )
    return [nn(half[:, k:], fac[k:, k : k + KMAX]) for k in range(0, m, KMAX)]


def kernel(
    slabs, patches, parts,
    r_hbm, l_hbm, f_hbm, b_hbm, margin_ref, out_ref,
    r_v, fac, maps,
    tail_s, head_s, zt_s, zh_s, d_s, u_s,
    tail_r, head_r, zt_r, zh_r, d_r, u_r,
    adj, acc, gt, opd, opu, place, zr,
    load_sem, send_sem, recv_sem, go_sem,
):
    s = lax.axis_index("slab")
    q = lax.axis_index("patch")
    left = lax.rem(q + patches - 1, patches)
    right = lax.rem(q + 1, patches)
    around = (left, right, q)
    m = fac.shape[-1]
    face = f_hbm.shape[-2]
    cols = r_v.shape[0]
    step = cols // parts
    first_slab, last_slab = s == 0, s == slabs - 1
    inner_low, inner_high = s > 0, s < slabs - 1

    loads = [
        pltpu.make_async_copy(r_hbm.at[0, 0], r_v, load_sem.at[0]),
        pltpu.make_async_copy(l_hbm.at[0, 0], fac, load_sem.at[1]),
        pltpu.make_async_copy(f_hbm.at[0, 0], maps.at[:face], load_sem.at[2]),
        pltpu.make_async_copy(b_hbm.at[0, 0], maps.at[face:], load_sem.at[3]),
    ]
    for c in loads:
        c.start()

    barrier = pltpu.get_barrier_semaphore()

    def greet(slab, patch):
        pl.semaphore_signal(barrier, inc=1, device_id=(slab, patch), device_id_type=MESH)

    greet(s, left)
    greet(s, right)

    @pl.when(inner_low)
    def _():
        for p in around:
            greet(s - 1, p)

    @pl.when(inner_high)
    def _():
        for p in around:
            greet(s + 1, p)

    slot = [0]

    def send(src, dst, slab, patch):
        n = slot[0]
        slot[0] += 1
        return pltpu.make_async_remote_copy(
            src_ref=src, dst_ref=dst, send_sem=send_sem.at[n], recv_sem=recv_sem.at[n],
            device_id=(slab, patch), device_id_type=MESH,
        )

    rows = [pl.ds(c * step, step) for c in range(parts)]
    tail_c = [send(tail_s.at[w], tail_r.at[w], s, right) for w in rows]
    head_c = [send(head_s.at[w], head_r.at[w], s, left) for w in rows]
    low_rows, high_rows = pl.ds(0, face), pl.ds(face, face)
    zd_c = [send(zt_s.at[low_rows], zt_r.at[low_rows], s, right), send(zh_s.at[low_rows], zh_r.at[low_rows], s, left)]
    zu_c = [send(zt_s.at[high_rows], zt_r.at[high_rows], s, right), send(zh_s.at[high_rows], zh_r.at[high_rows], s, left)]
    targets = ((2, left), (1, right), (0, q))
    down_c = [[send(d_s.at[w], d_r.at[j, w], s + 1, p) for j, p in targets] for w in rows]
    up_c = [[send(u_s.at[w], u_r.at[j, w], s - 1, p) for j, p in targets] for w in rows]

    count = margin_ref[0, 0]
    row = lax.broadcasted_iota(jnp.int32, (KMAX, KMAX), 0)
    col = lax.broadcasted_iota(jnp.int32, (KMAX, KMAX), 1)
    hit = (row == KMAX - count + col) & (col < count)
    place[...] = jnp.where(hit, 1.0, 0.0).astype(BF)

    loads[0].wait()
    loads[1].wait()
    first = solve(r_v[...].astype(BF), fac, m)
    tail_s[...] = nn(first[-1].astype(BF), place[...]).astype(BF)
    head_s[...] = first[0].astype(BF)

    pl.semaphore_wait(barrier, 2 + 3 * inner_low.astype(jnp.int32) + 3 * inner_high.astype(jnp.int32))

    def send_first():
        for a, b in zip(tail_c, head_c):
            a.start()
            b.start()

    @pl.when(s != 1)
    def _():
        send_first()

    loads[2].wait()
    loads[3].wait()
    for k, part in enumerate(solve(maps[...], fac, m)):
        gt[:, k * KMAX : (k + 1) * KMAX] = part.astype(BF)

    low = fac[:, :face]
    high = fac[m - face :, m - face :]
    k_tail = jnp.concatenate(
        [tn(low[m - KMAX :], fac[m - KMAX :, m - KMAX :]), tn(high, fac[m - face :, m - KMAX :])], axis=0
    )
    k_head = jnp.concatenate([tn(low, fac[:, :KMAX]), tn(high, fac[m - face :, :KMAX])], axis=0)
    zt_s[...] = nn(k_tail.astype(BF), place[...]).astype(BF)
    zh_s[...] = k_head.astype(BF)

    @pl.when(s == 1)
    def _():
        pl.semaphore_wait(go_sem, 1)
        send_first()

    @pl.when(inner_low)
    def _():
        for c in zd_c:
            c.start()

    @pl.when(inner_low & inner_high)
    def _():
        for c in zu_c:
            c.start()

    def send_down(c):
        w = rows[c]
        d_s[w] = acc[w, :face].astype(BF)
        for x in down_c[c]:
            x.start()

    def send_up(c):
        w = rows[c]
        u_s[w] = acc[w, face:].astype(BF)
        for x in up_c[c]:
            x.start()

    for c, w in enumerate(rows):
        tail_c[c].wait_recv()
        head_c[c].wait_recv()
        adj[w, :] = r_v[w, :]
        adj[w, :KMAX] = adj[w, :KMAX] - 0.5 * tail_r[w].astype(F32)
        adj[w, m - KMAX :] = adj[w, m - KMAX :] - 0.5 * nt(head_r[w], place[...])
        acc[w, :face] = nt(adj[w, :].astype(BF), gt[:face])

        @pl.when(first_slab)
        def _():
            send_down(c)
            tail_c[c].wait_send()
            head_c[c].wait_send()
            if c == 0:
                pl.semaphore_signal(go_sem, inc=1, device_id=(s + 1, q), device_id_type=MESH)

    @pl.when(first_slab)
    def _():
        for c in zu_c:
            c.start()

    acc[:, face:] = nt(adj[...].astype(BF), gt[face:])

    @pl.when(inner_low)
    def _():
        for c in zd_c:
            c.wait_recv()
        zr[low_rows] = nt(zh_r[low_rows], place[...]).astype(BF)
        opd[:face, :] = (-gt[:, :face].astype(F32)).T.astype(BF)
        opd[face : 2 * face, :] = (0.5 * nt(zt_r[low_rows], gt[:, :KMAX])).astype(BF)
        opd[2 * face :, :] = (0.5 * nt(zr[low_rows], gt[:, m - KMAX :])).astype(BF)

    def make_up():
        for c in zu_c:
            c.wait_recv()
        zr[high_rows] = nt(zh_r[high_rows], place[...]).astype(BF)

        @pl.when(inner_low)
        def _():
            opu[:face, :] = (-gt[face:, m - face :].astype(F32)).T.astype(BF)
            opu[face : 2 * face, :] = (0.5 * nt(zt_r[high_rows], gt[face:, :KMAX])).astype(BF)
            opu[2 * face :, :] = (0.5 * nt(zr[high_rows], gt[face:, m - KMAX :])).astype(BF)

    def beside(ref, w):
        return jnp.concatenate([ref[0, w], ref[1, w], ref[2, w]], axis=1)

    @pl.when(inner_low)
    def _():
        for c, w in enumerate(rows):
            for x in down_c[c]:
                x.wait_recv()

            @pl.when(inner_high)
            def _():
                acc[w, :face] += nn(beside(d_r, w), opd[:, :face])
                send_down(c)

            @pl.when(last_slab)
            def _():
                acc[w, face:] += nn(beside(d_r, w), opd[:, face:])
                send_up(c)

        @pl.when(inner_high)
        def _():
            every = pl.ds(0, cols)
            acc[:, face:] += nn(beside(d_r, every), opd[:, face:])

        adj[:, :face] = adj[:, :face] - d_r[0].astype(F32)
        adj[:, :KMAX] = adj[:, :KMAX] + 0.5 * nn(d_r[1], zt_r[low_rows])
        adj[:, m - KMAX :] = adj[:, m - KMAX :] + 0.5 * nn(d_r[2], zr[low_rows])

    @pl.when(inner_high)
    def _():
        make_up()
        for c, w in enumerate(rows):
            for x in up_c[c]:
                x.wait_recv()

            @pl.when(inner_low)
            def _():
                acc[w, face:] += nn(beside(u_r, w), opu[...])
                send_up(c)

        adj[:, m - face :] = adj[:, m - face :] - u_r[0].astype(F32)
        adj[:, :KMAX] = adj[:, :KMAX] + 0.5 * nn(u_r[1], zt_r[high_rows])
        adj[:, m - KMAX :] = adj[:, m - KMAX :] + 0.5 * nn(u_r[2], zr[high_rows])

    for k, part in enumerate(solve(adj[...].astype(BF), fac, m)):
        out_ref[0, 0, :, k * KMAX : (k + 1) * KMAX] = part

    @pl.when(inner_low)
    def _():
        for c in tail_c + head_c + zd_c:
            c.wait_send()
        for group in up_c:
            for x in group:
                x.wait_send()

    @pl.when(inner_high)
    def _():
        for c in zu_c:
            c.wait_send()
        for group in down_c:
            for x in group:
                x.wait_send()


def on_device(slabs, patches, right_side, inverse_factor, forward_trace, backward_trace, margin):
    cols, m = right_side.shape[2:]
    face = forward_trace.shape[2]
    parts = 2
    copies = 2 * parts + 4 + 6 * parts
    wide = pltpu.VMEM((cols, KMAX), BF)
    square = pltpu.VMEM((2 * face, KMAX), BF)
    thin = pltpu.VMEM((cols, face), BF)
    three = pltpu.VMEM((3, cols, face), BF)
    hbm = pl.BlockSpec(memory_space=pltpu.HBM)
    return pl.pallas_call(
        functools.partial(kernel, slabs, patches, parts),
        out_shape=jax.ShapeDtypeStruct(right_side.shape, F32),
        in_specs=[hbm, hbm, hbm, hbm, pl.BlockSpec(memory_space=pltpu.SMEM)],
        out_specs=pl.BlockSpec(memory_space=pltpu.VMEM),
        scratch_shapes=[
            pltpu.VMEM((cols, m), F32),
            pltpu.VMEM((m, m), BF),
            pltpu.VMEM((2 * face, m), BF),
            wide, wide, square, square, thin, thin,
            wide, wide, square, square, three, three,
            pltpu.VMEM((cols, m), F32),
            pltpu.VMEM((cols, 2 * face), F32),
            pltpu.VMEM((2 * face, m), BF),
            pltpu.VMEM((3 * face, 2 * face), BF),
            pltpu.VMEM((3 * face, face), BF),
            pltpu.VMEM((KMAX, KMAX), BF),
            square,
            pltpu.SemaphoreType.DMA((4,)),
            pltpu.SemaphoreType.DMA((copies,)),
            pltpu.SemaphoreType.DMA((copies,)),
            pltpu.SemaphoreType.REGULAR,
        ],
        compiler_params=pltpu.CompilerParams(collective_id=0, has_side_effects=True),
        name="sweeps",
    )(right_side, inverse_factor, forward_trace, backward_trace, margin)


def solution(mesh):
    four = P("slab", "patch", None, None)
    return jax.shard_map(
        functools.partial(on_device, mesh.shape["slab"], mesh.shape["patch"]),
        mesh=mesh,
        in_specs=(four, four, four, four, P("slab", "patch")),
        out_specs=four,
        check_vma=False,
    )
```

time: 49.1 us -> 47.3 us (0.963)
  Pallas kernels: 46.1 us -> 44.4 us
    pallas_call x1, Pallas kernels: 46.1 us -> 44.4 us  [on_device(): pl.pallas_call(functools.partial(kernel, slabs, patches, parts), out_shap...]
where the time goes in v2:
time: 47.3 us; the launch traced here: 47.1 us
  Pallas kernels  44.4 us (94%)
  local copies, waits for them, and re-layouts  2.06 us (4%)
  between operations  0.66 us (1%)
    pallas_call x1, Pallas kernels, on_device(): pl.pallas_call(functools.partial(kernel, slabs, patches, parts), out_shap...  44.4 us
    unnamed x1, local copies, waits for them, and re-layouts  2.06 us

profile of v2, /device:TPU:0, one launch (start us, length us, event | category | flops | bytes accessed | tf_op | source)
XLA Modules:
  0.0 47.1 jit_solution(1769471507620177631)
XLA Ops:
  0.7 44.4 %sweeps.1 = f32[1,1,256,768]{3,2,1,0:T(8,128)} custom-call(f32[1,1,256,768]{3,2,1,0:T(8,128)} %r_hbm.1, bf16[1,1,768,768]{3,2,1,0:T(8,128)(2,1)} %l_hbm.1, bf16[1,1,128,768]{3,2,1,0:T(8,128)(2,1)} %f_hbm.1, bf16[1,1,128,768]{3,2,1,0:T(8,128)(2,1)} %b_hbm.1, s32[1,1]{1,0:T(1,128)S(6)} %copy.7.margin_ref), custom_call_target="tpu_custom_call" | custom-call | tf_op jit(solution)/shard_map/sweeps/pallas_call | solution.py:285
  45.1 2.1 %copy.8 = f32[1,1,256,768]{3,2,1,0:T(8,128)} copy(f32[1,1,256,768]{3,2,1,0:T(8,128)} %sweeps.1) | data formatting | bytes 1572864

commit v3 on v2

--- a/solution.py
+++ b/solution.py
@@ -40,7 +40,7 @@
     tail_s, head_s, zt_s, zh_s, d_s, u_s,
     tail_r, head_r, zt_r, zh_r, d_r, u_r,
     adj, acc, gt, opd, opu, place, zr,
-    load_sem, send_sem, recv_sem, go_sem,
+    load_sem, send_sem, recv_sem,
 ):
     s = lax.axis_index("slab")
     q = lax.axis_index("patch")
@@ -115,14 +115,9 @@
 
     pl.semaphore_wait(barrier, 2 + 3 * inner_low.astype(jnp.int32) + 3 * inner_high.astype(jnp.int32))
 
-    def send_first():
-        for a, b in zip(tail_c, head_c):
-            a.start()
-            b.start()
-
-    @pl.when(s != 1)
-    def _():
-        send_first()
+    for a, b in zip(tail_c, head_c):
+        a.start()
+        b.start()
 
     loads[2].wait()
     loads[3].wait()
@@ -138,11 +133,6 @@
     zt_s[...] = nn(k_tail.astype(BF), place[...]).astype(BF)
     zh_s[...] = k_head.astype(BF)
 
-    @pl.when(s == 1)
-    def _():
-        pl.semaphore_wait(go_sem, 1)
-        send_first()
-
     @pl.when(inner_low)
     def _():
         for c in zd_c:
@@ -176,10 +166,6 @@
         @pl.when(first_slab)
         def _():
             send_down(c)
-            tail_c[c].wait_send()
-            head_c[c].wait_send()
-            if c == 0:
-                pl.semaphore_signal(go_sem, inc=1, device_id=(s + 1, q), device_id_type=MESH)
 
     @pl.when(first_slab)
     def _():
@@ -255,9 +241,12 @@
     for k, part in enumerate(solve(adj[...].astype(BF), fac, m)):
         out_ref[0, 0, :, k * KMAX : (k + 1) * KMAX] = part
 
-    @pl.when(inner_low)
-    def _():
-        for c in tail_c + head_c + zd_c:
+    for c in tail_c + head_c:
+        c.wait_send()
+
+    @pl.when(inner_low)
+    def _():
+        for c in zd_c:
             c.wait_send()
         for group in up_c:
             for x in group:
@@ -275,7 +264,7 @@
 def on_device(slabs, patches, right_side, inverse_factor, forward_trace, backward_trace, margin):
     cols, m = right_side.shape[2:]
     face = forward_trace.shape[2]
-    parts = 2
+    parts = 4
     copies = 2 * parts + 4 + 6 * parts
     wide = pltpu.VMEM((cols, KMAX), BF)
     square = pltpu.VMEM((2 * face, KMAX), BF)
@@ -303,7 +292,6 @@
             pltpu.SemaphoreType.DMA((4,)),
             pltpu.SemaphoreType.DMA((copies,)),
             pltpu.SemaphoreType.DMA((copies,)),
-            pltpu.SemaphoreType.REGULAR,
         ],
         compiler_params=pltpu.CompilerParams(collective_id=0, has_side_effects=True),
         name="sweeps",

time: 47.3 us -> 44.2 us (0.934)
  Pallas kernels: 44.4 us -> 41.3 us
    pallas_call x1, Pallas kernels: 44.4 us -> 41.3 us  [on_device(): pl.pallas_call(functools.partial(kernel, slabs, patches, parts), out_shap...]
where the time goes in v3:
time: 44.2 us; the launch traced here: 44 us
  Pallas kernels  41.3 us (93%)
  local copies, waits for them, and re-layouts  2.06 us (5%)
  between operations  0.66 us (1%)
    pallas_call x1, Pallas kernels, on_device(): pl.pallas_call(functools.partial(kernel, slabs, patches, parts), out_shap...  41.3 us
    unnamed x1, local copies, waits for them, and re-layouts  2.06 us

profile of v3, /device:TPU:0, one launch (start us, length us, event | category | flops | bytes accessed | tf_op | source)
XLA Modules:
  0.0 44.0 jit_solution(11302119895105256224)
XLA Ops:
  0.7 41.3 %sweeps.1 = f32[1,1,256,768]{3,2,1,0:T(8,128)} custom-call(f32[1,1,256,768]{3,2,1,0:T(8,128)} %r_hbm.1, bf16[1,1,768,768]{3,2,1,0:T(8,128)(2,1)} %l_hbm.1, bf16[1,1,128,768]{3,2,1,0:T(8,128)(2,1)} %f_hbm.1, bf16[1,1,128,768]{3,2,1,0:T(8,128)(2,1)} %b_hbm.1, s32[1,1]{1,0:T(1,128)S(6)} %copy.7.margin_ref), custom_call_target="tpu_custom_call" | custom-call | tf_op jit(solution)/shard_map/sweeps/pallas_call | solution.py:274
  42.0 2.1 %copy.8 = f32[1,1,256,768]{3,2,1,0:T(8,128)} copy(f32[1,1,256,768]{3,2,1,0:T(8,128)} %sweeps.1) | data formatting | bytes 1572864

commit v4 on v3

--- a/solution.py
+++ b/solution.py
@@ -25,12 +25,27 @@
     return lax.dot_general(a, b, (((0,), (0,)), ((), ())), preferred_element_type=F32)
 
 
-def solve(x, fac, m):
-    half = jnp.concatenate(
+def halfway(x, fac, m):
+    return jnp.concatenate(
         [nt(x[:, : i + KMAX], fac[i : i + KMAX, : i + KMAX]).astype(BF) for i in range(0, m, KMAX)],
         axis=1,
     )
+
+
+def solve(x, fac, m):
+    half = halfway(x, fac, m)
     return [nn(half[:, k:], fac[k:, k : k + KMAX]) for k in range(0, m, KMAX)]
+
+
+def finish(half_ref, l_ref, out_ref, held, sem):
+    m = half_ref.shape[1]
+    copies = []
+    for n, k in enumerate(range(0, m, KMAX)):
+        held[n] = nn(half_ref[:, k:], l_ref[0, 0, k:, k : k + KMAX])
+        copies.append(pltpu.make_async_copy(held.at[n], out_ref.at[0, 0, :, k : k + KMAX], sem.at[n]))
+        copies[-1].start()
+    for c in copies:
+        c.wait()
 
 
 def kernel(
@@ -238,8 +253,7 @@
         adj[:, :KMAX] = adj[:, :KMAX] + 0.5 * nn(u_r[1], zt_r[high_rows])
         adj[:, m - KMAX :] = adj[:, m - KMAX :] + 0.5 * nn(u_r[2], zr[high_rows])
 
-    for k, part in enumerate(solve(adj[...].astype(BF), fac, m)):
-        out_ref[0, 0, :, k * KMAX : (k + 1) * KMAX] = part
+    out_ref[...] = halfway(adj[...].astype(BF), fac, m)
 
     for c in tail_c + head_c:
         c.wait_send()
@@ -271,9 +285,9 @@
     thin = pltpu.VMEM((cols, face), BF)
     three = pltpu.VMEM((3, cols, face), BF)
     hbm = pl.BlockSpec(memory_space=pltpu.HBM)
-    return pl.pallas_call(
+    half = pl.pallas_call(
         functools.partial(kernel, slabs, patches, parts),
-        out_shape=jax.ShapeDtypeStruct(right_side.shape, F32),
+        out_shape=jax.ShapeDtypeStruct((cols, m), BF),
         in_specs=[hbm, hbm, hbm, hbm, pl.BlockSpec(memory_space=pltpu.SMEM)],
         out_specs=pl.BlockSpec(memory_space=pltpu.VMEM),
         scratch_shapes=[
@@ -296,6 +310,15 @@
         compiler_params=pltpu.CompilerParams(collective_id=0, has_side_effects=True),
         name="sweeps",
     )(right_side, inverse_factor, forward_trace, backward_trace, margin)
+    return pl.pallas_call(
+        finish,
+        out_shape=jax.ShapeDtypeStruct(right_side.shape, F32),
+        in_specs=[pl.BlockSpec(memory_space=pltpu.VMEM)] * 2,
+        out_specs=hbm,
+        scratch_shapes=[pltpu.VMEM((m // KMAX, cols, KMAX), F32), pltpu.SemaphoreType.DMA((m // KMAX,))],
+        compiler_params=pltpu.CompilerParams(vmem_limit_bytes=16 << 20),
+        name="finish",
+    )(half, inverse_factor)
 
 
 def solution(mesh):

time: 44.2 us -> 43.4 us (0.982)
  local copies, waits for them, and re-layouts: 2.06 us -> 0.99 us
    pallas_call x0 -> x1, Pallas kernels: none -> 1.27 us  [on_device(): pl.pallas_call(finish, out_shape=jax.ShapeDtypeStruct(right_side.shape, F...]
    unnamed x1 -> x4, local copies, waits for them, and re-layouts: 2.06 us -> 0.99 us
    pallas_call x1, Pallas kernels: 41.3 us -> 40.3 us  [on_device(): pl.pallas_call(functools.partial(kernel, slabs, patches, parts), out_shap...]
where the time goes in v4:
time: 43.4 us; the launch traced here: 43.3 us
  Pallas kernels  41.6 us (96%)
  local copies, waits for them, and re-layouts  0.99 us (2%)
  between operations  0.68 us (2%)
    pallas_call x1, Pallas kernels, on_device(): pl.pallas_call(functools.partial(kernel, slabs, patches, parts), out_shap...  40.3 us
    pallas_call x1, Pallas kernels, on_device(): pl.pallas_call(finish, out_shape=jax.ShapeDtypeStruct(right_side.shape, F...  1.27 us
    unnamed x4, local copies, waits for them, and re-layouts  0.99 us

profile of v4, /device:TPU:0, one launch (start us, length us, event | category | flops | bytes accessed | tf_op | source)
XLA Modules:
  0.0 43.3 jit_solution(10343577973049957735)
XLA Ops:
  0.7 0.0 copy-start
  0.7 40.3 %sweeps.1.half_ref = bf16[256,768]{1,0:T(8,128)(2,1)} custom-call(f32[1,1,256,768]{3,2,1,0:T(8,128)} %r_hbm.1, bf16[1,1,768,768]{3,2,1,0:T(8,128)(2,1)} %l_ref.1, bf16[1,1,128,768]{3,2,1,0:T(8,128)(2,1)} %f_hbm.1, bf16[1,1,128,768]{3,2,1,0:T(8,128)(2,1)} %b_hbm.1, s32[1,1]{1,0:T(1,128)S(6)} %copy.6.margin_ref), custom_call_target="tpu_custom_call" | custom-call | tf_op jit(solution)/shard_map/sweeps/pallas_call | solution.py:288
  41.0 0.0 copy-done
  41.0 0.0 copy-start.1
  41.0 1.0 %copy-done.1 = bf16[256,768]{1,0:T(8,128)(2,1)S(1)} copy-done((bf16[256,768]{1,0:T(8,128)(2,1)S(1)}, bf16[256,768]{1,0:T(8,128)(2,1)}, u32[]{:S(2)}) %copy-start.1) | copy-done | bytes 393240
  42.0 1.3 %finish.1 = f32[1,1,256,768]{3,2,1,0:T(8,128)} custom-call(bf16[256,768]{1,0:T(8,128)(2,1)S(1)} %copy-done.1, bf16[1,1,768,768]{3,2,1,0:T(8,128)(2,1)S(1)} %copy-done), custom_call_target="tpu_custom_call" | custom-call | tf_op jit(solution)/shard_map/finish/pallas_call | solution.py:313
Async XLA Ops:
  0.7 40.3 %copy-start = (bf16[1,1,768,768]{3,2,1,0:T(8,128)(2,1)S(1)}, bf16[1,1,768,768]{3,2,1,0:T(8,128)(2,1)}, u32[]{:S(2)}) copy-start(bf16[1,1,768,768]{3,2,1,0:T(8,128)(2,1)} %l_ref.1) | copy-start | bytes 3538948
  41.0 1.0 %copy-start.1 = (bf16[256,768]{1,0:T(8,128)(2,1)S(1)}, bf16[256,768]{1,0:T(8,128)(2,1)}, u32[]{:S(2)}) copy-start(bf16[256,768]{1,0:T(8,128)(2,1)} %sweeps.1.half_ref) | copy-start | bytes 1179652

commit v5 on v4

--- a/solution.py
+++ b/solution.py
@@ -249,9 +249,9 @@
                 acc[w, face:] += nn(beside(u_r, w), opu[...])
                 send_up(c)
 
-        adj[:, m - face :] = adj[:, m - face :] - u_r[0].astype(F32)
-        adj[:, :KMAX] = adj[:, :KMAX] + 0.5 * nn(u_r[1], zt_r[high_rows])
-        adj[:, m - KMAX :] = adj[:, m - KMAX :] + 0.5 * nn(u_r[2], zr[high_rows])
+            adj[w, m - face :] = adj[w, m - face :] - u_r[0, w].astype(F32)
+            adj[w, :KMAX] = adj[w, :KMAX] + 0.5 * nn(u_r[1, w], zt_r[high_rows])
+            adj[w, m - KMAX :] = adj[w, m - KMAX :] + 0.5 * nn(u_r[2, w], zr[high_rows])
 
     out_ref[...] = halfway(adj[...].astype(BF), fac, m)
 

time: 43.4 us -> 43.4 us (level)
  no operation moved by 1% of the time
where the time goes in v5:
time: 43.4 us; the launch traced here: 43.2 us
  Pallas kernels  41.5 us (96%)
  local copies, waits for them, and re-layouts  0.99 us (2%)
  between operations  0.68 us (2%)
    pallas_call x1, Pallas kernels, on_device(): pl.pallas_call(functools.partial(kernel, slabs, patches, parts), out_shap...  40.3 us
    pallas_call x1, Pallas kernels, on_device(): pl.pallas_call(finish, out_shape=jax.ShapeDtypeStruct(right_side.shape, F...  1.27 us
    unnamed x4, local copies, waits for them, and re-layouts  0.99 us

profile of v5, /device:TPU:0, one launch (start us, length us, event | category | flops | bytes accessed | tf_op | source)
XLA Modules:
  0.0 43.2 jit_solution(7206255783285314177)
XLA Ops:
  0.7 0.0 copy-start
  0.7 40.3 %sweeps.1.half_ref = bf16[256,768]{1,0:T(8,128)(2,1)} custom-call(f32[1,1,256,768]{3,2,1,0:T(8,128)} %r_hbm.1, bf16[1,1,768,768]{3,2,1,0:T(8,128)(2,1)} %l_ref.1, bf16[1,1,128,768]{3,2,1,0:T(8,128)(2,1)} %f_hbm.1, bf16[1,1,128,768]{3,2,1,0:T(8,128)(2,1)} %b_hbm.1, s32[1,1]{1,0:T(1,128)S(6)} %copy.6.margin_ref), custom_call_target="tpu_custom_call" | custom-call | tf_op jit(solution)/shard_map/sweeps/pallas_call | solution.py:288
  40.9 0.0 copy-done
  40.9 0.0 copy-start.1
  40.9 1.0 %copy-done.1 = bf16[256,768]{1,0:T(8,128)(2,1)S(1)} copy-done((bf16[256,768]{1,0:T(8,128)(2,1)S(1)}, bf16[256,768]{1,0:T(8,128)(2,1)}, u32[]{:S(2)}) %copy-start.1) | copy-done | bytes 393240
  41.9 1.3 %finish.1 = f32[1,1,256,768]{3,2,1,0:T(8,128)} custom-call(bf16[256,768]{1,0:T(8,128)(2,1)S(1)} %copy-done.1, bf16[1,1,768,768]{3,2,1,0:T(8,128)(2,1)S(1)} %copy-done), custom_call_target="tpu_custom_call" | custom-call | tf_op jit(solution)/shard_map/finish/pallas_call | solution.py:313
Async XLA Ops:
  0.7 40.3 %copy-start = (bf16[1,1,768,768]{3,2,1,0:T(8,128)(2,1)S(1)}, bf16[1,1,768,768]{3,2,1,0:T(8,128)(2,1)}, u32[]{:S(2)}) copy-start(bf16[1,1,768,768]{3,2,1,0:T(8,128)(2,1)} %l_ref.1) | copy-start | bytes 3538948
  40.9 1.0 %copy-start.1 = (bf16[256,768]{1,0:T(8,128)(2,1)S(1)}, bf16[256,768]{1,0:T(8,128)(2,1)}, u32[]{:S(2)}) copy-start(bf16[256,768]{1,0:T(8,128)(2,1)} %sweeps.1.half_ref) | copy-start | bytes 1179652
